TPU v7x, 128 devices: a whole 4x4x4 slice. The times are simulated.
128 devices in a mesh: lat: 4 (over x), ord: 16 (over y, z), batch: 2 (over core).
Axes of the slice: x: 4, y: 4, z: 4, core: 2. Of those that a mesh axis runs over, the one named last changes fastest.
Arguments:
- state_field: bfloat16 [512, 720, 1440], P(('batch', 'ord'), 'lat'), parts along dimension 0, may hold values from -6 to 6
- slot_order: int32 [512], replicated, may hold values from 0 to 511, each once
- legendre: bfloat16 [512, 720, 720], P(('lat', 'ord')), may hold values from -0.21875 to 0.21875
- degree_gain: float32 [720, 256], replicated, may hold values from 0.25 to 1.75
- mixing: bfloat16 [256, 256], replicated, may hold values from -0.375 to 0.375
Outputs:
- updated: bfloat16 [512, 720, 1440], P(('batch', 'ord'), 'lat'), parts along dimension 0
There are 2 independent parts, one for each index of `batch`. A program takes and returns all parts, laid end to end along the dimension named above; an argument that names none is the same for every part. Nothing has to cross between parts.
Inputs may be any that keep to these rules, and one draw needn't show every extreme that they name: `slot_order`: each of 0 to 511 stands once.
All inputs are finite; a program needn't handle non-finite values.
Results may differ from a plain program's by a relative error of at most 0.0054.
Values may be sent and summed in bfloat16 or wider, within the bound.
A program may use at most 192 MiB of HBM per device.

v0:
```python
import math

import jax
import jax.numpy as jnp
from jax import lax
from jax.sharding import PartitionSpec as P


def tables(orders, lon_count):
    longitude = jnp.arange(lon_count, dtype=jnp.int32)
    phase = orders[:, None] * longitude[None, :] % lon_count
    angle = phase.astype(jnp.float32) * (2.0 * math.pi / lon_count)
    root = 1.0 / math.sqrt(lon_count)
    cosine = jnp.cos(angle)
    sine = jnp.sin(angle)
    forward = jnp.stack([cosine * root, -sine * root], axis=1).astype(jnp.bfloat16)
    weights = jnp.where(orders == 0, 1.0, 2.0).astype(jnp.float32) * root
    inverse = jnp.stack([cosine * weights[:, None], -sine * weights[:, None]], axis=1).astype(
        jnp.bfloat16
    )
    return (forward, inverse)


def shards(state_field, slot_order, legendre, degree_gain, mixing):
    channels, lat_rows, lon_count = state_field.shape
    all_slots = slot_order.shape[0]
    my_slots, degrees, latitudes = legendre.shape
    width = mixing.shape[0]
    lat_count = lax.axis_size("lat")
    ord_count = lax.axis_size("ord")
    forward, inverse = tables(slot_order, lon_count)
    fourier = lax.dot_general(
        forward.reshape(2 * all_slots, lon_count),
        state_field.reshape(channels * lat_rows, lon_count),
        (((1,), (1,)), ((), ())),
        preferred_element_type=jnp.float32,
    )
    fourier = fourier.astype(jnp.bfloat16)
    arrived = lax.all_to_all(
        fourier.reshape(1, all_slots, 2, channels, lat_rows),
        ("lat", "ord"),
        split_axis=1,
        concat_axis=0,
        tiled=True,
    )
    arrived = arrived.reshape(lat_count, ord_count, my_slots, 2, channels, lat_rows).transpose(
        2, 3, 1, 4, 0, 5
    )
    gathered = arrived.reshape(my_slots, 2 * width, latitudes)
    orders_here = lax.dynamic_slice_in_dim(
        slot_order, lax.axis_index(("lat", "ord")) * my_slots, my_slots, 0
    )
    padded_gain = jnp.concatenate([degree_gain, jnp.zeros((degrees, width), jnp.float32)], axis=0)
    spec = jnp.einsum("sjl,sxl->sjx", legendre, gathered, preferred_element_type=jnp.float32)

    def pick_rows(order_value):
        return lax.dynamic_slice_in_dim(padded_gain, order_value, degrees, 0)

    gain_rows = jax.vmap(pick_rows)(orders_here)
    kept = jnp.arange(degrees, dtype=jnp.int32)[None, :] < (degrees - orders_here)[:, None]
    filtered = jnp.where(
        kept[:, :, None, None],
        spec.reshape(my_slots, degrees, 2, width) * gain_rows[:, :, None, :],
        0.0,
    )
    filtered = filtered.astype(jnp.bfloat16)
    mixed = jnp.dot(
        filtered.reshape(my_slots * degrees * 2, width), mixing, preferred_element_type=jnp.float32
    )
    mixed = mixed.astype(jnp.bfloat16).reshape(my_slots, degrees, 2 * width)
    synth = jnp.einsum("sjx,sjl->sxl", mixed, legendre, preferred_element_type=jnp.float32).astype(
        jnp.bfloat16
    )
    outgoing = synth.reshape(my_slots, 2, ord_count, channels, lat_count, lat_rows).transpose(
        4, 2, 0, 1, 3, 5
    )
    outgoing = outgoing.reshape(lat_count * ord_count, my_slots, 2, channels, lat_rows)
    returned = lax.all_to_all(outgoing, ("lat", "ord"), split_axis=0, concat_axis=0, tiled=True)
    returned = returned.reshape(2 * all_slots, channels * lat_rows)
    back = lax.dot_general(
        returned,
        inverse.reshape(2 * all_slots, lon_count),
        (((0,), (0,)), ((), ())),
        preferred_element_type=jnp.float32,
    )
    back = back.reshape(channels, lat_rows, lon_count)
    return (state_field.astype(jnp.float32) + jax.nn.gelu(back, approximate=True)).astype(
        jnp.bfloat16
    )


def solution(mesh):
    placed = (P(("batch", "ord"), "lat", None), P(), P(("lat", "ord"), None, None), P(), P())
    return jax.shard_map(
        shards,
        mesh=mesh,
        in_specs=placed,
        out_specs=P(("batch", "ord"), "lat", None),
        check_vma=False,
    )
```

profile of v0, /device:TPU:82, one launch (start us, length us, event | category | flops | bytes accessed | tf_op | source)
XLA Modules:
  0.0 555.5 jit_solution(5158348730062671081)
XLA Ops:
  0.0 0.7 select_multiply_fusion
  0.7 14.0 %multiply_convert_fusion.1 = (bf16[512,1,1440]{0,2,1:T(8,128)(2,1)S(1)}, bf16[512,1,1440]{0,2,1:T(8,128)(2,1)S(1)}, bf16[512,1,1440]{0,2,1:T(8,128)(2,1)S(1)}, bf16[512,1,1440]{0,2,1:T(8,128)(2,1)S(1)}) fusion(f32[512]{0:T(512)S(1)} %select_multiply_fusion, s32[512]{0:T(512)} %param.6), kind=kLoop, calls=%fused_computation.28 | loop fusion | flops 13271040 | bytes 5902336 | tf_op jit(solution)/shard_map/convert
  14.7 2.9 pad_maximum_fusion
  17.6 7.4 %copy.33 = bf16[512,2,1440]{2,1,0:T(2,128)(2,1)S(1)} copy(bf16[512,2,1440]{0,2,1:T(8,128)(2,1)} %get-tuple-element.27) | data formatting | bytes 5898240 | tf_op jit(solution)/shard_map/stack | solution.py:16
  25.0 3.6 convert_element_type.65
  28.6 11.9 %copy.34 = bf16[16,180,1440]{2,1,0:T(8,128)(2,1)} copy(bf16[16,180,1440]{2,0,1:T(8,128)(2,1)} %param.5) | data formatting | bytes 16588800 | tf_op args[0]
  40.5 10.9 %reshape.240 = bf16[2880,1440]{1,0:T(8,128)(2,1)} reshape(bf16[16,180,1440]{2,1,0:T(8,128)(2,1)} %copy.34) | data formatting | bytes 16588800 | tf_op jit(solution)/shard_map/reshape | solution.py:34
  51.4 13.9 %convolution_convert_fusion.1 = bf16[1024,2880]{0,1:T(8,128)(2,1)} fusion(bf16[1024,1440]{1,0:T(8,128)(2,1)S(1)} %copy-done.2, bf16[2880,1440]{1,0:T(8,128)(2,1)} %reshape.240), kind=kOutput, calls=%fused_computation.17 | convolution fusion | flops 8496414720 | bytes 17141760 | tf_op jit(solution)/shard_map/dot_general | solution.py:32
  65.3 8.5 %copy.35 = bf16[1024,2880]{1,0:T(8,128)(2,1)} copy(bf16[1024,2880]{0,1:T(8,128)(2,1)} %convolution_convert_fusion.1) | data formatting | bytes 11796480 | tf_op jit(solution)/shard_map/convert_element_type | solution.py:38
  73.8 27.5 %reshape.241 = bf16[1,512,2,16,180]{4,3,2,1,0:T(8,128)(2,1)} reshape(bf16[1024,2880]{1,0:T(8,128)(2,1)} %copy.35) | data formatting | bytes 11796480 | tf_op jit(solution)/shard_map/reshape | solution.py:40
  101.3 11.1 %all-to-all-start = ((bf16[1,512,2,16,180]{4,3,2,0,1:T(8,128)(2,1)}), bf16[1,512,2,16,180]{4,3,2,0,1:T(8,128)(2,1)}, u32[]{:S(2)}, u32[]{:S(2)}) async-start(bf16[1,512,2,16,180]{4,3,2,0,1:T(8,128)(2,1)} %bitcast.34), calls=%async_computation | async-start | bytes 16777216 | tf_op jit(solution)/shard_map/all_to_all | solution.py:39
  112.4 0.8 broadcast_subtract_fusion
  113.3 17.8 %while.1 = (s32[]{:T(128)}, f32[1440,256]{1,0:T(8,128)S(1)}, s32[8,2]{0,1:T(2,128)S(1)}, f32[8,720,256]{2,1,0:T(8,128)}, s32[]{:T(128)}) while((s32[]{:T(128)}, f32[1440,256]{1,0:T(8,128)S(1)}, s32[8,2]{0,1:T(2,128)S(1)}, f32[8,720,256]{2,1,0:T(8,128)}, s32[]{:T(128)}) %tuple.21), condition=%wide.while_cond, body=%wide.while_body.sunk | while | flops 2 | bytes 1475173 | solution.py:57
  113.4 0.6 slice.12
  114.0 1.6 bitcast_dynamic-update-slice_fusion.2
  115.6 0.6 slice.12
  116.2 1.6 bitcast_dynamic-update-slice_fusion.2
  117.9 0.6 slice.12
  118.4 1.6 bitcast_dynamic-update-slice_fusion.2
  120.7 1.6 bitcast_dynamic-update-slice_fusion.2
  122.9 1.6 bitcast_dynamic-update-slice_fusion.2
  125.1 1.6 bitcast_dynamic-update-slice_fusion.2
  127.3 1.6 bitcast_dynamic-update-slice_fusion.2
  129.5 1.6 bitcast_dynamic-update-slice_fusion.2
  131.1 13.0 %mul.158 = f32[8,720,2,256]{3,2,1,0:T(2,128)} broadcast(f32[8,720,256]{2,1,0:T(8,128)} %get-tuple-element.12), dimensions={0,1,3} | broadcast | bytes 17694720 | tf_op jit(solution)/shard_map/mul | solution.py:63
  144.2 14.9 %mul.159 = f32[11520,256]{1,0:T(8,128)} reshape(f32[8,720,2,256]{3,2,1,0:T(2,128)} %mul.158) | data formatting | bytes 23592960 | tf_op jit(solution)/shard_map/mul | solution.py:63
  159.1 1.5 broadcast_in_dim.36
  160.6 2.4 broadcast_in_dim.37
  163.1 70.9 %all-to-all-done = bf16[1,512,2,16,180]{4,3,2,0,1:T(8,128)(2,1)} async-done(((bf16[1,512,2,16,180]{4,3,2,0,1:T(8,128)(2,1)}), bf16[1,512,2,16,180]{4,3,2,0,1:T(8,128)(2,1)}, u32[]{:S(2)}, u32[]{:S(2)}) %all-to-all-start) | async-done | bytes 5898272 | tf_op jit(solution)/shard_map/all_to_all | solution.py:39
  234.0 12.1 %copy.56 = bf16[4,16,8,2,16,180]{5,0,4,1,3,2:T(4,128)(2,1)} copy(bf16[4,16,8,2,16,180]{5,4,3,2,1,0:T(8,128)(2,1)} %bitcast.1) | data formatting | bytes 11796480 | tf_op jit(solution)/shard_map/reshape | solution.py:46
  246.1 15.3 %reshape.243 = bf16[8,512,720]{2,1,0:T(8,128)(2,1)} reshape(bf16[8,2,16,16,4,180]{5,4,3,2,1,0:T(4,128)(2,1)} %bitcast.35) | data formatting | bytes 11796480 | tf_op jit(solution)/shard_map/reshape | solution.py:49
  261.4 14.4 %convolution_bitcast_fusion = f32[8,720,512]{2,1,0:T(8,128)} fusion(bf16[8,512,720]{2,1,0:T(8,128)(2,1)} %reshape.243, bf16[8,720,720]{2,1,0:T(8,128)(2,1)} %param.7), kind=kOutput, calls=%fused_computation.19 | convolution fusion | flops 4246732800 | bytes 25989120 | tf_op jit(solution)/shard_map/sjl,sxl->sjx/dot_general | solution.py:54
  275.8 13.5 %reshape.244 = f32[11520,256]{1,0:T(8,128)} reshape(f32[8,720,512]{2,1,0:T(8,128)} %convolution_bitcast_fusion) | data formatting | bytes 23592960 | tf_op jit(solution)/shard_map/reshape | solution.py:63
  289.3 13.5 %convolution_convert_fusion = bf16[11520,256]{1,0:T(8,128)(2,1)} fusion(bf16[256,256]{1,0:T(8,128)(2,1)S(1)} %copy-done, f32[11520,256]{1,0:T(8,128)} %reshape.244, f32[11520,256]{1,0:T(8,128)} %mul.159, pred[11520]{0:T(1024)(128)(4,1)S(1)} %broadcast_in_dim.37), kind=kOutput, calls=%fused_computation.12 | convolution fusion | flops 1521745920 | bytes 29633792 | tf_op jit(solution)/shard_map/dot_general | solution.py:67
  302.8 9.7 %reshape.245 = bf16[8,720,512]{2,1,0:T(8,128)(2,1)} reshape(bf16[11520,256]{1,0:T(8,128)(2,1)} %convolution_convert_fusion) | data formatting | bytes 11796480 | tf_op jit(solution)/shard_map/reshape | solution.py:70
  312.5 11.8 %convolution_convert_fusion.2 = bf16[8,512,720]{1,2,0:T(8,128)(2,1)} fusion(bf16[8,720,512]{2,1,0:T(8,128)(2,1)} %reshape.245, bf16[8,720,720]{2,1,0:T(8,128)(2,1)} %param.7), kind=kOutput, calls=%fused_computation.20 | convolution fusion | flops 4249681920 | bytes 20090880 | tf_op jit(solution)/shard_map/sjx,sjl->sxl/dot_general | solution.py:71
  324.3 8.4 %copy.40 = bf16[8,512,720]{2,1,0:T(8,128)(2,1)} copy(bf16[8,512,720]{1,2,0:T(8,128)(2,1)} %convolution_convert_fusion.2) | data formatting | bytes 11796480 | tf_op jit(solution)/shard_map/convert_element_type | solution.py:71
  332.7 18.0 %reshape.246 = bf16[8,2,16,16,4,180]{5,4,3,2,1,0:T(4,128)(2,1)} reshape(bf16[8,512,720]{2,1,0:T(8,128)(2,1)} %copy.40) | data formatting | bytes 11796480 | tf_op jit(solution)/shard_map/reshape | solution.py:74
  350.8 8.2 %copy.41 = bf16[4,16,8,2,16,180]{5,4,3,2,1,0:T(8,128)(2,1)} copy(bf16[4,16,8,2,16,180]{5,0,4,1,3,2:T(4,128)(2,1)} %bitcast.36) | data formatting | bytes 11796480 | tf_op jit(solution)/shard_map/transpose | solution.py:74
  359.0 9.5 %all-to-all-start.1 = ((bf16[64,8,2,16,180]{4,3,2,1,0:T(8,128)(2,1)}), bf16[64,8,2,16,180]{4,3,2,1,0:T(8,128)(2,1)}, u32[]{:S(2)}, u32[]{:S(2)}) async-start(bf16[64,8,2,16,180]{4,3,2,1,0:T(8,128)(2,1)} %bitcast.37), calls=%async_computation.1 | async-start | bytes 16777216 | tf_op jit(solution)/shard_map/all_to_all | solution.py:78
  368.6 7.4 %copy.43 = bf16[512,2,1440]{2,1,0:T(2,128)(2,1)S(1)} copy(bf16[512,2,1440]{0,2,1:T(8,128)(2,1)} %get-tuple-element.28) | data formatting | bytes 5898240 | tf_op jit(solution)/shard_map/stack | solution.py:18
  376.0 3.5 convert_element_type.70
  379.6 111.9 %all-to-all-done.1 = bf16[64,8,2,16,180]{4,3,2,1,0:T(8,128)(2,1)} async-done(((bf16[64,8,2,16,180]{4,3,2,1,0:T(8,128)(2,1)}), bf16[64,8,2,16,180]{4,3,2,1,0:T(8,128)(2,1)}, u32[]{:S(2)}, u32[]{:S(2)}) %all-to-all-start.1) | async-done | bytes 5898272 | tf_op jit(solution)/shard_map/all_to_all | solution.py:78
  491.5 15.6 %reshape.248 = bf16[1024,2880]{1,0:T(8,128)(2,1)} reshape(bf16[64,8,2,16,180]{4,3,2,1,0:T(8,128)(2,1)} %all-to-all-done.1) | data formatting | bytes 11796480 | tf_op jit(solution)/shard_map/reshape | solution.py:79
  507.1 8.4 %copy.42 = bf16[2880,1024]{1,0:T(8,128)(2,1)} copy(bf16[2880,1024]{0,1:T(8,128)(2,1)} %bitcast.38) | data formatting | bytes 11796480 | tf_op jit(solution)/shard_map/dot_general | solution.py:80
  515.5 8.0 %dot_general.27 = bf16[16,180,1024]{2,1,0:T(8,128)(2,1)} reshape(bf16[2880,1024]{1,0:T(8,128)(2,1)} %copy.42) | data formatting | bytes 11796480 | tf_op jit(solution)/shard_map/dot_general | solution.py:80
  523.5 16.3 %fusion.11 = f32[16,180,1440]{2,1,0:T(8,128)} fusion(bf16[16,180,1024]{2,1,0:T(8,128)(2,1)} %dot_general.27, bf16[1024,1440]{1,0:T(8,128)(2,1)} %convert_element_type.70), kind=kOutput, calls=%fused_computation.21 | convolution fusion | flops 8493465600 | bytes 25436160 | tf_op jit(solution)/shard_map/dot_general | solution.py:80
  539.8 15.3 %fusion.8 = bf16[16,180,1440]{2,0,1:T(8,128)(2,1)} fusion(f32[16,180,1440]{2,1,0:T(8,128)} %fusion.11, bf16[16,180,1440]{2,0,1:T(8,128)(2,1)S(1)} %bitcast.33), kind=kLoop, calls=%fused_computation.11 | loop fusion | flops 45619200 | bytes 33177600 | tf_op jit(solution)/shard_map/convert_element_type | solution.py:87
  (32 shorter events, 3.7 us)
Async XLA Ops:
  0.0 289.3 %copy-start = (bf16[256,256]{1,0:T(8,128)(2,1)S(1)}, bf16[256,256]{1,0:T(8,128)(2,1)}, u32[]{:S(2)}) copy-start(bf16[256,256]{1,0:T(8,128)(2,1)} %param.9) | copy-start | bytes 393220
  40.5 10.9 %copy-start.2 = (bf16[1024,1440]{1,0:T(8,128)(2,1)S(1)}, bf16[1024,1440]{1,0:T(8,128)(2,1)}, u32[]{:S(2)}) copy-start(bf16[1024,1440]{1,0:T(8,128)(2,1)} %convert_element_type.65) | copy-start | bytes 8847364
  101.3 11.9 %copy-start.3 = (f32[720,256]{1,0:T(8,128)S(1)}, f32[720,256]{1,0:T(8,128)}, u32[]{:S(2)}) copy-start(f32[720,256]{1,0:T(8,128)} %param.8) | copy-start | bytes 2211844
  101.3 132.7 %all-to-all-start = ((bf16[1,512,2,16,180]{4,3,2,0,1:T(8,128)(2,1)}), bf16[1,512,2,16,180]{4,3,2,0,1:T(8,128)(2,1)}, u32[]{:S(2)}, u32[]{:S(2)}) async-start(bf16[1,512,2,16,180]{4,3,2,0,1:T(8,128)(2,1)} %bitcast.34), calls=%async_computation | async-start | bytes 16777216 | tf_op jit(solution)/shard_map/all_to_all | solution.py:39
  359.0 132.5 %all-to-all-start.1 = ((bf16[64,8,2,16,180]{4,3,2,1,0:T(8,128)(2,1)}), bf16[64,8,2,16,180]{4,3,2,1,0:T(8,128)(2,1)}, u32[]{:S(2)}, u32[]{:S(2)}) async-start(bf16[64,8,2,16,180]{4,3,2,1,0:T(8,128)(2,1)} %bitcast.37), calls=%async_computation.1 | async-start | bytes 16777216 | tf_op jit(solution)/shard_map/all_to_all | solution.py:78
  515.5 24.3 %slice-start = ((s8[8847360]{0:T(1024)(128)(4,1)}), s8[458752]{0:T(1024)(128)(4,1)S(1)}, s32[]{:S(2)}) async-start(s8[8847360]{0:T(1024)(128)(4,1)} %bitcast.32), calls=%async_computation.2 | async-start | bytes 917504
  523.5 16.3 %slice-start.1 = ((s8[8847360]{0:T(1024)(128)(4,1)}), s8[4194304]{0:T(1024)(128)(4,1)S(1)}, s32[]{:S(2)}) async-start(s8[8847360]{0:T(1024)(128)(4,1)} %bitcast.32), calls=%async_computation.3 | async-start | bytes 8388608
  523.5 16.3 %slice-start.2 = ((s8[8847360]{0:T(1024)(128)(4,1)}), s8[4194304]{0:T(1024)(128)(4,1)S(1)}, s32[]{:S(2)}) async-start(s8[8847360]{0:T(1024)(128)(4,1)} %bitcast.32), calls=%async_computation.4 | async-start | bytes 8388608
  539.8 15.3 %copy-start.1 = (bf16[256,256]{1,0:T(8,128)(2,1)S(1)}, bf16[256,256]{1,0:T(8,128)(2,1)}, u32[]{:S(2)}) copy-start(bf16[256,256]{1,0:T(8,128)(2,1)} %param.9) | copy-start | bytes 393220
where the time goes:
time: 566 us; the launch traced here: 556 us
  local copies, waits for them, and re-layouts  248 us (44%)
  waiting for transfers between devices  183 us (32%)
  matrix products  69.9 us (12%)
  other arithmetic  33.7 us (6%)
  starting transfers between devices  20.6 us (4%)
    all_to_all x1, waiting for transfers between devices, shards(): lax.all_to_all(outgoing, ('lat', 'ord'), split_axis=0, concat_axis=0, til...  112 us
    all_to_all x1, waiting for transfers between devices, shards(): lax.all_to_all(fourier.reshape(1, all_slots, 2, channels, lat_rows), ('la...  70.9 us
    mul x2, local copies, waits for them, and re-layouts, shards(): spec.reshape(my_slots, degrees, 2, width) * gain_rows[:, :, None, :]  27.9 us
    reshape x1, local copies, waits for them, and re-layouts, shards(): fourier.reshape(1, all_slots, 2, channels, lat_rows)  27.5 us
    reshape x1, local copies, waits for them, and re-layouts, shards(): synth.reshape(my_slots, 2, ord_count, channels, lat_count, lat_rows)  18 us
    gather x24, local copies, waits for them, and re-layouts  17.8 us
    dot_general x2, local copies, waits for them, and re-layouts, shards(): lax.dot_general(returned, inverse.reshape(2 * all_slots, lon_count), (((0...  16.4 us
    dot_general x1, matrix products, shards(): lax.dot_general(returned, inverse.reshape(2 * all_slots, lon_count), (((0...  16.3 us
  transfers between devices with their start and end apart: 2, of which 2 were waited for; matrix products, arithmetic and copies ran while one was open for 11% of the time, Pallas kernels for 0%

commit v1 on v0

v1 whole, which is shorter than its diff:
```python
import functools
import math

import jax
import jax.numpy as jnp
from jax import lax
from jax.experimental import pallas as pl
from jax.experimental.pallas import tpu as pltpu
from jax.sharding import PartitionSpec as P

MESH = pl.DeviceIdType.MESH
BF = jnp.bfloat16
F32 = jnp.float32
LON = 1440
LONP = 1536
NX = 4
NO = 16
ND = NX * NO
MY = 8
PAIRS = 8
LAT = 180
DEG = 720
WIDE = 768
VLIM = 64 * 2**20 - 65536


def nn(a, b):
    return lax.dot_general(a, b, (((1,), (0,)), ((), ())), preferred_element_type=F32)


def nt(a, b):
    return lax.dot_general(a, b, (((1,), (1,)), ((), ())), preferred_element_type=F32)


def one_hot(cond):
    return jnp.where(cond, 1.0, 0.0).astype(BF)


def iota(shape, dim):
    return lax.broadcasted_iota(jnp.int32, shape, dim)


def cos_phase(p):
    p = p - jnp.floor(p * (1.0 / LON)) * LON
    a = (jnp.abs(p - LON / 2) - LON / 4) * (2.0 * math.pi / LON)
    z = a * a
    s = -1.0 / 39916800.0
    for c in (1.0 / 362880.0, -1.0 / 5040.0, 1.0 / 120.0, -1.0 / 6.0):
        s = s * z + c
    return a + a * (z * s)


def shuffle_matrix(transposed):
    i = iota((256, 256), 1 if transposed else 0)
    j = iota((256, 256), 0 if transposed else 1)
    src = (i % 8) * 32 + (i // 16) * 2 + (i // 8) % 2
    return one_hot(src == j)


def prologue_kernel(m_ref, gain_ref, mix_ref, gains_ref, mix2_ref):
    for i in range(MY):
        m = m_ref[i]
        rows = gain_ref[pl.ds(pl.multiple_of(m // 8 * 8, 8), WIDE + 8), :]
        rows = pltpu.roll(rows, lax.rem(WIDE + 8 - lax.rem(m, 8), WIDE + 8), 0)[0:WIDE]
        t = rows.T * jnp.where(m == 0, 1.0, 2.0)
        for h in range(2):
            for o in range(NO):
                at = (h * NO + o) * 8
                gains_ref[i, at : at + 8, :] = t[o * 16 + h * 8 : o * 16 + h * 8 + 8, :]
    i = iota((512, 256), 0)
    c = (i // 16) % NO * 16 + (i // 256) * 8 + i % 8
    j = iota((512, 256), 1)
    acc = jnp.zeros((512, 512), F32)
    for r in range(2):
        e = one_hot((c == j) & ((i // 8) % 2 == r))
        half = nt(e, mix_ref[...]).astype(BF)
        acc = acc + nt(half, e)
    mix2_ref[...] = acc.astype(BF)


def prologue(orders_here, degree_gain, mixing):
    padded = jnp.pad(degree_gain, ((0, 1288 - DEG), (0, 0)))
    vm = pl.BlockSpec(memory_space=pltpu.VMEM)
    return pl.pallas_call(
        prologue_kernel,
        out_shape=(
            jax.ShapeDtypeStruct((MY, 256, WIDE), F32),
            jax.ShapeDtypeStruct((512, 512), BF),
        ),
        in_specs=[pl.BlockSpec(memory_space=pltpu.SMEM), vm, vm],
        out_specs=(vm, vm),
        compiler_params=pltpu.CompilerParams(vmem_limit_bytes=VLIM),
        name="prologue",
    )(orders_here, padded, mixing)


def make_table(m_ref, f_ref):
    n = m_ref.shape[0]
    m = m_ref[...].astype(F32)
    r = (iota((n, 1), 0) % 2).astype(F32) * (LON / 4)
    low = m * iota((n, 128), 1).astype(F32) + r
    high = m * (iota((n, 128), 1) * 128).astype(F32)
    root = 1.0 / math.sqrt(LON)
    c0, s0 = cos_phase(low) * root, cos_phase(low + 0.75 * LON) * root
    c1, s1 = cos_phase(high), cos_phase(high + 0.75 * LON)
    lane = iota((1, 128), 1)
    for t in range(LONP // 128):
        v = c0 * c1[:, t : t + 1] - s0 * s1[:, t : t + 1]
        if t == LONP // 128 - 1:
            v = jnp.where(lane < LON - t * 128, v, 0.0)
        f_ref[:, t * 128 : (t + 1) * 128] = v.astype(BF)


def fill_grid(x_ref, xb):
    xb[:, :, LON:] = jnp.zeros((PAIRS, 384, LONP - LON), BF)
    xb[:, 304:320, :] = jnp.zeros((PAIRS, 16, LONP), BF)
    xb[:, 368:384, :] = jnp.zeros((PAIRS, 16, LONP), BF)

    def body(p, _):
        for h in range(2):
            xb[p, h * 128 : h * 128 + 128, 0:LON] = x_ref[h * 8 + p, 0:128, :]
            at = 256 + 64 * h
            xb[p, at : at + 52, 0:LON] = x_ref[h * 8 + p, 128:180, :]
        return 0

    lax.fori_loop(0, PAIRS, body, 0)


def forward_chunk(g, f_ref, xb, yb, send_ref, shuffle):
    rows = f_ref[pl.ds(pl.multiple_of(g * 256, 256), 256), :]

    def body(p, _):
        y = nt(rows, xb[p]).astype(BF)
        for q in range(8):
            yb[q, pl.ds(pl.multiple_of(p * 32, 32), 32), :] = y[q * 32 : q * 32 + 32, :]
        return 0

    lax.fori_loop(0, PAIRS, body, 0)
    for q in range(8):
        send_ref[2 * g + q // 4, q % 4] = nn(shuffle, yb[q]).astype(BF)


def forward_kernel(m_ref, x_ref, send_ref, f_ref, xb, yb):
    make_table(m_ref, f_ref)
    fill_grid(x_ref, xb)
    shuffle = shuffle_matrix(False)

    def body(g, _):
        forward_chunk(g, f_ref, xb, yb, send_ref, shuffle)
        return 0

    lax.fori_loop(0, 4, body, 0)


def forward(order_rows, state):
    vm = pl.BlockSpec(memory_space=pltpu.VMEM)
    return pl.pallas_call(
        forward_kernel,
        out_shape=(
            jax.ShapeDtypeStruct((MY, NX, 256, 384), BF),
            jax.ShapeDtypeStruct((2 * MY * ND, LONP), BF),
        ),
        in_specs=[vm, vm],
        out_specs=(vm, vm),
        scratch_shapes=[
            pltpu.VMEM((PAIRS, 384, LONP), BF),
            pltpu.VMEM((8, 256, 384), BF),
        ],
        compiler_params=pltpu.CompilerParams(vmem_limit_bytes=VLIM),
        name="forward",
    )(order_rows, state)


def greet():
    barrier = pltpu.get_barrier_semaphore()
    me = lax.axis_index("lat") * NO + lax.axis_index("ord")

    def body(k, _):
        d = lax.rem(me + k, ND)
        pl.semaphore_signal(
            barrier,
            inc=1,
            device_id={"lat": d // NO, "ord": lax.rem(d, NO)},
            device_id_type=MESH,
        )
        return 0

    lax.fori_loop(1, ND, body, 0)
    pl.semaphore_wait(barrier, ND - 1)


def partner(k, x, o):
    y, z = o // 4, lax.rem(o, 4)
    dx = lax.rem(x + k // 16, 4)
    dy = lax.rem(y + lax.rem(k // 4, 4), 4)
    dz = lax.rem(z + lax.rem(k, 4), 4)
    return dx, dy * 4 + dz


def send_slot(s, src, dst, send_sem, recv_sem, own_sem):
    x, o = lax.axis_index("lat"), lax.axis_index("ord")
    me = x * NO + o

    def body(k, _):
        dx, do = partner(k, x, o)
        pltpu.make_async_remote_copy(
            src_ref=src.at[s, dx * NO + do],
            dst_ref=dst.at[s, me],
            send_sem=send_sem,
            recv_sem=recv_sem.at[s],
            device_id={"lat": dx, "ord": do},
            device_id_type=MESH,
        ).start()
        return 0

    lax.fori_loop(1, ND, body, 0)
    pltpu.make_async_copy(src.at[s, me], dst.at[s, me], own_sem.at[s]).start()


def wait_slot(s, dst, recv_sem, own_sem):
    me = lax.axis_index("lat") * NO + lax.axis_index("ord")
    pltpu.make_async_copy(dst.at[s, me], dst.at[s, me], own_sem.at[s]).wait()
    others = dst.at[s, 0 : ND - 1]
    pltpu.make_async_copy(others, others, recv_sem.at[s]).wait()


def wait_sent(src, send_sem):
    others = src.at[:, 0 : ND - 1]
    pltpu.make_async_copy(others, others, send_sem).wait()


def exchange_kernel(src, dst, send_sem, recv_sem, own_sem):
    greet()
    for s in range(MY):
        send_slot(s, src, dst, send_sem, recv_sem, own_sem)
    for s in range(MY):
        wait_slot(s, dst, recv_sem, own_sem)
    wait_sent(src, send_sem)


def exchange(a, which):
    hbm = pl.BlockSpec(memory_space=pl.ANY)
    return pl.pallas_call(
        exchange_kernel,
        out_shape=jax.ShapeDtypeStruct(a.shape, a.dtype),
        in_specs=[hbm],
        out_specs=hbm,
        scratch_shapes=[
            pltpu.SemaphoreType.DMA,
            pltpu.SemaphoreType.DMA((MY,)),
            pltpu.SemaphoreType.DMA((MY,)),
        ],
        compiler_params=pltpu.CompilerParams(collective_id=which, has_side_effects=True),
        name=f"exchange_{which}",
    )(a)


def lat_select():
    row = iota((DEG, WIDE), 0)
    n = iota((DEG, WIDE), 1)
    tail = n - 512
    main = (n // 128) * LAT + n % 128
    rest = jnp.where(tail % 64 < 52, (tail // 64) * LAT + 128 + tail % 64, -1)
    return one_hot(row == jnp.where(n < 512, main, rest))


def slot_math(got, leg, gain, mix2, out):
    lane = iota((1, 128), 1)
    parts = [got(x) for x in range(NX)]
    rest = [v[:, 256:384].astype(F32) for v in parts]
    turned = [pltpu.roll(v, 64, 1) for v in rest]
    halves = []
    for h in range(2):
        cols = [v[:, h * 128 : h * 128 + 128] for v in parts]
        for x in (0, 2):
            a = rest[x] if h == 0 else turned[x]
            b = turned[x + 1] if h == 0 else rest[x + 1]
            cols.append(jnp.where(lane < 64, a, b).astype(BF))
        spec = nt(jnp.concatenate(cols, axis=1), leg)
        spec = spec.reshape(NO, 2, 8, WIDE) * gain[h * 128 : h * 128 + 128].reshape(NO, 1, 8, WIDE)
        halves.append(spec.reshape(256, WIDE).astype(BF))
    filtered = jnp.concatenate(halves, axis=0)
    syn = []
    for h in range(2):
        mixed = nn(mix2[h * 256 : h * 256 + 256], filtered).astype(BF)
        syn.append(nn(mixed, leg))
    for x in range(NX):
        at = 512 + (x // 2) * 128
        a, b = syn[0][:, at : at + 128], syn[1][:, at : at + 128]
        if x % 2:
            a = pltpu.roll(a, 64, 1)
        else:
            b = pltpu.roll(b, 64, 1)
        cols = [v[:, x * 128 : x * 128 + 128] for v in syn] + [jnp.where(lane < 64, a, b)]
        out(x, jnp.concatenate(cols, axis=1).astype(BF))


def middle_kernel(g_ref, leg_ref, gain_ref, mix2_ref, s_ref, legp, select):
    @pl.when(pl.program_id(0) == 0)
    def _():
        legp[DEG:WIDE, :] = jnp.zeros((WIDE - DEG, WIDE), BF)
        select[...] = lat_select()

    legp[0:DEG, :] = nn(leg_ref[0], select[...]).astype(BF)

    def out(x, v):
        s_ref[0, x] = v

    slot_math(lambda x: g_ref[0, x], legp[...], gain_ref[0], mix2_ref[...], out)


def middle(g, legendre, gains, mix2):
    block = pl.BlockSpec((1, NX, 256, 384), lambda i: (i, 0, 0, 0))
    return pl.pallas_call(
        middle_kernel,
        grid=(MY,),
        out_shape=jax.ShapeDtypeStruct(g.shape, BF),
        in_specs=[
            block,
            pl.BlockSpec((1, DEG, DEG), lambda i: (i, 0, 0)),
            pl.BlockSpec((1, 256, WIDE), lambda i: (i, 0, 0)),
            pl.BlockSpec((512, 512), lambda i: (0, 0)),
        ],
        out_specs=block,
        scratch_shapes=[pltpu.VMEM((WIDE, WIDE), BF), pltpu.VMEM((DEG, WIDE), BF)],
        compiler_params=pltpu.CompilerParams(vmem_limit_bytes=VLIM),
        name="middle",
    )(g, legendre, gains, mix2)


def inverse_kernel(r_ref, f_ref, x_ref, out_ref, b):
    @pl.when(pl.program_id(0) == 0)
    def _():
        shuffle = shuffle_matrix(True)

        def body(i, _):
            v = nn(shuffle, r_ref[i // NX, lax.rem(i, NX)]).astype(BF)
            for p in range(PAIRS):
                b[p, pl.ds(pl.multiple_of(i * 32, 32), 32), :] = v[p * 32 : p * 32 + 32, :]
            return 0

        lax.fori_loop(0, MY * NX, body, 0)

    bt = b[pl.program_id(0)].T
    for n in range(3):
        lanes = slice(n * 512, min(n * 512 + 512, LON))
        back = nn(bt, f_ref[:, n * 512 : n * 512 + 512])[:, : lanes.stop - lanes.start]
        back = jax.nn.gelu(back, approximate=True)
        for h in range(2):
            for rows, at in ((slice(0, 128), h * 128), (slice(128, 180), 256 + 64 * h)):
                size = rows.stop - rows.start
                x = x_ref[h, 0, rows, lanes].astype(F32)
                out_ref[h, 0, rows, lanes] = (x + back[at : at + size]).astype(BF)


def inverse(r, f, state):
    grid_block = pl.BlockSpec((2, 1, LAT, LON), lambda p: (0, p, 0, 0))
    whole = lambda shape: pl.BlockSpec(shape, lambda p: (0,) * len(shape))
    out = pl.pallas_call(
        inverse_kernel,
        grid=(PAIRS,),
        out_shape=jax.ShapeDtypeStruct((2, PAIRS, LAT, LON), BF),
        in_specs=[whole(r.shape), whole(f.shape), grid_block],
        out_specs=grid_block,
        scratch_shapes=[pltpu.VMEM((PAIRS, 2 * MY * ND, 384), BF)],
        compiler_params=pltpu.CompilerParams(vmem_limit_bytes=VLIM),
        name="inverse",
    )(r, f, state.reshape(2, PAIRS, LAT, LON))
    return out.reshape(2 * PAIRS, LAT, LON)


def shards(state_field, slot_order, legendre, degree_gain, mixing):
    me = lax.axis_index(("lat", "ord"))
    orders_here = lax.dynamic_slice_in_dim(slot_order, me * MY, MY, 0)
    order_rows = jnp.repeat(slot_order.reshape(ND, MY).T.reshape(-1), 2)[:, None]
    gains, mix2 = prologue(orders_here, degree_gain, mixing)
    send, table = forward(order_rows, state_field)
    got = exchange(send.reshape(MY, ND, 16, 384), 0).reshape(send.shape)
    answer = middle(got, legendre, gains, mix2)
    returned = exchange(answer.reshape(MY, ND, 16, 384), 1).reshape(send.shape)
    return inverse(returned, table, state_field)


def solution(mesh):
    placed = (P(("batch", "ord"), "lat", None), P(), P(("lat", "ord"), None, None), P(), P())
    return jax.shard_map(
        shards,
        mesh=mesh,
        in_specs=placed,
        out_specs=P(("batch", "ord"), "lat", None),
        check_vma=False,
    )
```

time: 566 us -> 286 us (0.51)
  the two profiles are of different devices: /device:TPU:82 before, /device:TPU:0 now
where the time goes in v1:
time: 286 us; the launch traced here: 285 us
  Pallas kernels  258 us (90%)
  local copies, waits for them, and re-layouts  27.6 us (10%)
    pallas_call x2, Pallas kernels, exchange(): pl.pallas_call(exchange_kernel, out_shape=jax.ShapeDtypeStruct(a.shape, a...  159 us
    pallas_call x1, Pallas kernels, forward(): pl.pallas_call(forward_kernel, out_shape=(jax.ShapeDtypeStruct((MY, NX, 2...  34.6 us
    pallas_call x1, Pallas kernels, middle(): pl.pallas_call(middle_kernel, grid=(MY,), out_shape=jax.ShapeDtypeStruct(...  28.6 us
    pallas_call x1, Pallas kernels, inverse(): pl.pallas_call(inverse_kernel, grid=(PAIRS,), out_shape=jax.ShapeDtypeStr...  27.4 us
    unnamed x1, local copies, waits for them, and re-layouts  11.9 us
    reshape x1, local copies, waits for them, and re-layouts, inverse(): return out.reshape(2 * PAIRS, LAT, LON)  10.1 us
    pallas_call x1, Pallas kernels, prologue(): pl.pallas_call(prologue_kernel, out_shape=(jax.ShapeDtypeStruct((MY, 256,...  8.31 us

profile of v1, /device:TPU:0, one launch (start us, length us, event | category | flops | bytes accessed | tf_op | source)
XLA Modules:
  0.0 285.3 jit_solution(9781500067062547812)
XLA Ops:
  0.0 1.3 dynamic_slice.3.m_ref
  1.3 0.8 reshape.24
  2.1 0.1 copy.9
  2.1 0.1 reshape.25
  2.2 0.1 broadcast_in_dim.3
  2.4 1.0 broadcast_in_dim_reshape.4.m_ref
  3.3 2.3 pad.4.gain_ref
  5.6 8.3 %prologue.1 = (f32[8,256,768]{2,1,0:T(8,128)}, bf16[512,512]{1,0:T(8,128)(2,1)}) custom-call(s32[8]{0:T(128)} %dynamic_slice.3.m_ref, f32[1288,256]{1,0:T(8,128)} %pad.4.gain_ref, bf16[256,256]{1,0:T(8,128)(2,1)} %mix_ref.1), custom_call_target="tpu_custom_call" | custom-call | tf_op jit(solution)/shard_map/prologue/pallas_call | solution.py:84
  13.9 11.9 %copy.11.x_ref = bf16[16,180,1440]{2,1,0:T(8,128)(2,1)} copy(bf16[16,180,1440]{2,0,1:T(8,128)(2,1)} %param.5) | data formatting | bytes 16588800 | tf_op args[0]
  25.8 34.6 %forward.1 = (bf16[8,4,256,384]{3,2,1,0:T(8,128)(2,1)}, bf16[1024,1536]{1,0:T(8,128)(2,1)}) custom-call(s32[1024,1]{1,0:T(8,128)} %broadcast_in_dim_reshape.4.m_ref, bf16[16,180,1440]{2,1,0:T(8,128)(2,1)} %copy.11.x_ref), custom_call_target="tpu_custom_call" | custom-call | tf_op jit(solution)/shard_map/forward/pallas_call | solution.py:157
  60.4 81.4 %exchange_0.1 = bf16[8,64,16,384]{3,2,1,0:T(8,128)(2,1)} custom-call(bf16[8,64,16,384]{3,2,1,0:T(8,128)(2,1)} %bitcast.12), custom_call_target="tpu_custom_call" | custom-call | tf_op jit(solution)/shard_map/exchange_0/pallas_call | solution.py:243
  141.8 28.6 %middle.1 = bf16[8,4,256,384]{3,2,1,0:T(8,128)(2,1)} custom-call(bf16[8,4,256,384]{3,2,1,0:T(8,128)(2,1)} %bitcast.9, bf16[8,720,720]{2,1,0:T(8,128)(2,1)} %leg_ref.1, f32[8,256,768]{2,1,0:T(8,128)} %get-tuple-element.10.gain_ref, bf16[512,512]{1,0:T(8,128)(2,1)} %get-tuple-element.11.mix2_ref), custom_call_target="tpu_custom_call" | custom-call | tf_op jit(solution)/shard_map/middle/pallas_call | solution.py:314
  170.4 77.4 %exchange_1.1 = bf16[8,64,16,384]{3,2,1,0:T(8,128)(2,1)} custom-call(bf16[8,64,16,384]{3,2,1,0:T(8,128)(2,1)} %bitcast.10), custom_call_target="tpu_custom_call" | custom-call | tf_op jit(solution)/shard_map/exchange_1/pallas_call | solution.py:243
  247.8 27.4 %inverse.1 = bf16[2,8,180,1440]{3,2,1,0:T(8,128)(2,1)} custom-call(bf16[8,4,256,384]{3,2,1,0:T(8,128)(2,1)} %bitcast.11, bf16[1024,1536]{1,0:T(8,128)(2,1)} %get-tuple-element.12.f_ref, bf16[2,8,180,1440]{3,2,1,0:T(8,128)(2,1)} %bitcast.7), custom_call_target="tpu_custom_call" | custom-call | tf_op jit(solution)/shard_map/inverse/pallas_call | solution.py:359
  275.2 10.1 %copy.13 = bf16[16,180,1440]{2,0,1:T(8,128)(2,1)} copy(bf16[16,180,1440]{2,1,0:T(8,128)(2,1)} %bitcast.8) | data formatting | bytes 16588800 | tf_op jit(solution)/shard_map/reshape | solution.py:369

commit v2 on v1

v2 whole, which is shorter than its diff:
```python
import functools
import math

import jax
import jax.numpy as jnp
from jax import lax
from jax.experimental import pallas as pl
from jax.experimental.pallas import tpu as pltpu
from jax.sharding import PartitionSpec as P

MESH = pl.DeviceIdType.MESH
BF = jnp.bfloat16
F32 = jnp.float32
LON = 1440
LONP = 1536
NX = 4
NO = 16
ND = NX * NO
MY = 8
PAIRS = 8
LAT = 180
DEG = 720
WIDE = 768
VLIM = 64 * 2**20 - 65536


def nn(a, b):
    return lax.dot_general(a, b, (((1,), (0,)), ((), ())), preferred_element_type=F32)


def nt(a, b):
    return lax.dot_general(a, b, (((1,), (1,)), ((), ())), preferred_element_type=F32)


def one_hot(cond):
    return jnp.where(cond, 1.0, 0.0).astype(BF)


def iota(shape, dim):
    return lax.broadcasted_iota(jnp.int32, shape, dim)


def cos_phase(p):
    p = p - jnp.floor(p * (1.0 / LON)) * LON
    a = (jnp.abs(p - LON / 2) - LON / 4) * (2.0 * math.pi / LON)
    z = a * a
    s = -1.0 / 39916800.0
    for c in (1.0 / 362880.0, -1.0 / 5040.0, 1.0 / 120.0, -1.0 / 6.0):
        s = s * z + c
    return a + a * (z * s)


def shuffle_matrix(transposed):
    i = iota((256, 256), 1 if transposed else 0)
    j = iota((256, 256), 0 if transposed else 1)
    src = (i % 8) * 32 + (i // 16) * 2 + (i // 8) % 2
    return one_hot(src == j)


def greet_signal():
    barrier = pltpu.get_barrier_semaphore()
    me = lax.axis_index("lat") * NO + lax.axis_index("ord")

    def body(k, _):
        d = lax.rem(me + k, ND)
        pl.semaphore_signal(
            barrier,
            inc=1,
            device_id={"lat": d // NO, "ord": lax.rem(d, NO)},
            device_id_type=MESH,
        )
        return 0

    lax.fori_loop(1, ND, body, 0)


def greet_wait():
    pl.semaphore_wait(pltpu.get_barrier_semaphore(), ND - 1)


def partner(k, x, o):
    y, z = o // 4, lax.rem(o, 4)
    dx = lax.rem(x + k // 16, 4)
    dy = lax.rem(y + lax.rem(k // 4, 4), 4)
    dz = lax.rem(z + lax.rem(k, 4), 4)
    return dx, dy * 4 + dz


def send_slot(s, src, dst, send_sem, recv_sem, own_sem):
    x, o = lax.axis_index("lat"), lax.axis_index("ord")
    me = x * NO + o

    def body(k, _):
        dx, do = partner(k, x, o)
        pltpu.make_async_remote_copy(
            src_ref=src.at[s, dx * NO + do],
            dst_ref=dst.at[s, me],
            send_sem=send_sem,
            recv_sem=recv_sem.at[s],
            device_id={"lat": dx, "ord": do},
            device_id_type=MESH,
        ).start()
        return 0

    lax.fori_loop(1, ND, body, 0)
    pltpu.make_async_copy(src.at[s, me], dst.at[s, me], own_sem.at[s]).start()


def wait_slot(s, dst, recv_sem, own_sem):
    me = lax.axis_index("lat") * NO + lax.axis_index("ord")
    pltpu.make_async_copy(dst.at[s, me], dst.at[s, me], own_sem.at[s]).wait()
    others = dst.at[s, 0 : ND - 1]
    pltpu.make_async_copy(others, others, recv_sem.at[s]).wait()


def wait_sent(src, send_sem):
    others = src.at[:, 0 : ND - 1]
    pltpu.make_async_copy(others, others, send_sem).wait()


def lat_select():
    row = iota((DEG, WIDE), 0)
    n = iota((DEG, WIDE), 1)
    tail = n - 512
    main = (n // 128) * LAT + n % 128
    rest = jnp.where(tail % 64 < 52, (tail // 64) * LAT + 128 + tail % 64, -1)
    return one_hot(row == jnp.where(n < 512, main, rest))


def slot_math(got, leg, gain, mix2, out):
    lane = iota((1, 128), 1)
    parts = [got(x) for x in range(NX)]
    rest = [v[:, 256:384].astype(F32) for v in parts]
    turned = [pltpu.roll(v, 64, 1) for v in rest]
    halves = []
    for h in range(2):
        cols = [v[:, h * 128 : h * 128 + 128] for v in parts]
        for x in (0, 2):
            a = rest[x] if h == 0 else turned[x]
            b = turned[x + 1] if h == 0 else rest[x + 1]
            cols.append(jnp.where(lane < 64, a, b).astype(BF))
        spec = nt(jnp.concatenate(cols, axis=1), leg)
        spec = spec.reshape(NO, 2, 8, WIDE) * gain[h * 128 : h * 128 + 128].reshape(NO, 1, 8, WIDE)
        halves.append(spec.reshape(256, WIDE).astype(BF))
    filtered = jnp.concatenate(halves, axis=0)
    syn = []
    for h in range(2):
        mixed = nn(mix2[h * 256 : h * 256 + 256, :], filtered).astype(BF)
        syn.append(nn(mixed, leg))
    for x in range(NX):
        at = 512 + (x // 2) * 128
        a, b = syn[0][:, at : at + 128], syn[1][:, at : at + 128]
        if x % 2:
            a = pltpu.roll(a, 64, 1)
        else:
            b = pltpu.roll(b, 64, 1)
        cols = [v[:, x * 128 : x * 128 + 128] for v in syn] + [jnp.where(lane < 64, a, b)]
        out(x, jnp.concatenate(cols, axis=1).astype(BF))


def swap_matrix():
    i = iota((256, 256), 0)
    j = iota((256, 256), 1)
    return one_hot((i % 16) * 16 + i // 16 == j)


def lat_rows(g, h):
    return h * 128 + g * 16 if g < 8 else 256 + h * 64 + (g - 8) * 16


def table_columns(order_ref):
    rep = one_hot(iota((128, ND), 0) // 2 == iota((128, ND), 1))
    m = order_ref[...]
    low = nn(rep, (m % 256).astype(F32).astype(BF))
    high = nn(rep, (m // 256).astype(F32).astype(BF))
    return low + 256.0 * high


def make_table(s, columns, f_ref):
    m = columns[:, s : s + 1]
    r = (iota((128, 1), 0) % 2).astype(F32) * (LON / 4)
    low = m * iota((128, 128), 1).astype(F32) + r
    high = m * (iota((128, 128), 1) * 128).astype(F32)
    root = 1.0 / math.sqrt(LON)
    c0, s0 = cos_phase(low) * root, cos_phase(low + 0.75 * LON) * root
    c1, s1 = cos_phase(high), cos_phase(high + 0.75 * LON)
    lane = iota((1, 128), 1)
    for t in range(LONP // 128):
        v = c0 * c1[:, t : t + 1] - s0 * s1[:, t : t + 1]
        if t == LONP // 128 - 1:
            v = jnp.where(lane < LON - t * 128, v, 0.0)
        f_ref[s * 128 : s * 128 + 128, t * 128 : (t + 1) * 128] = v.astype(BF)


def fill_grid(xs, xb, swap):
    def body(g, _):
        v = nn(swap, xs[pl.ds(g * 16, 16)].reshape(256, LON)).astype(BF)
        for c in range(16):
            h = c // 8
            at = jnp.where(g < 8, h * 128 + g * 16, 256 + h * 64 + (g - 8) * 16)
            xb[c % 8, pl.ds(pl.multiple_of(at, 16), 16), 0:LON] = v[c * 16 : c * 16 + 16]
        return 0

    lax.fori_loop(0, 12, body, 0)


def forward_chunk(g, f_ref, xb, yb, send, shuffle):
    rows = f_ref[pl.ds(pl.multiple_of(g * 256, 256), 256), :]

    def body(p, _):
        y = nt(rows, xb[p]).astype(BF)
        for q in range(8):
            yb[q, pl.ds(pl.multiple_of(p * 32, 32), 32), :] = y[q * 32 : q * 32 + 32, :]
        return 0

    lax.fori_loop(0, PAIRS, body, 0)
    for q in range(8):
        v = nn(shuffle, yb[q]).astype(BF)
        send[2 * g + q // 4, (q % 4) * 16 : (q % 4) * 16 + 16] = v.reshape(16, 16, 384)


def split_gain(gain_ref, gp):
    gp[:, DEG:] = jnp.zeros((768, WIDE - DEG), BF)
    t = gain_ref[...].T
    for piece in range(3):
        part = t.astype(BF)
        t = t - part.astype(F32)
        for h in range(2):
            for o in range(NO):
                at = piece * 256 + (h * NO + o) * 8
                gp[at : at + 8, 0:DEG] = part[o * 16 + h * 8 : o * 16 + h * 8 + 8, :]


def slot_gain(m, gp, gs):
    pick = one_hot(iota((WIDE, WIDE), 0) == iota((WIDE, WIDE), 1) + m)
    v = nn(gp[...], pick)
    weight = jnp.where(jnp.full((1, WIDE), m, jnp.int32) == 0, 1.0, 2.0)
    gs[...] = (v[0:256] + v[256:512] + v[512:768]) * weight


def two_part_mixing(mix_ref, mix2):
    i = iota((512, 256), 0)
    c = (i // 16) % NO * 16 + (i // 256) * 8 + i % 8
    j = iota((512, 256), 1)
    acc = jnp.zeros((512, 512), F32)
    for r in range(2):
        e = one_hot(c + 256 * ((i // 8) % 2) == j + 256 * r)
        half = nt(e, mix_ref[...]).astype(BF)
        acc = acc + nt(half, e)
    mix2[...] = acc.astype(BF)


def collect(s, ret, bb, tb, lb, shuffle_back, swap):
    for x in range(NX):
        v = nn(shuffle_back, ret[s, x * 16 : x * 16 + 16].reshape(256, 384)).astype(BF)
        for p in range(PAIRS):
            bb[p, x * 32 : x * 32 + 32, :] = v[p * 32 : p * 32 + 32, :]

    def turn(p, _):
        t = bb[p].T
        for h in range(2):
            for g in range(12):
                at = lat_rows(g, h)
                tb[g, pl.ds(pl.multiple_of(h * 128 + p * 16, 16), 16), :] = t[at : at + 16]
        return 0

    lax.fori_loop(0, PAIRS, turn, 0)

    def place(g, _):
        lb[pl.ds(pl.multiple_of(g * 256, 256), 256), :] = nn(swap, tb[g]).astype(BF)
        return 0

    lax.fori_loop(0, 12, place, 0)


def transform_kernel(
    so_ref, order_ref, gain_ref, mix_ref, x_hbm, leg_hbm,
    l_hbm, f_hbm,
    xs, xb, fb, yb, send, got, ans, ret, leg, legp, select, gp, gs, mix2, bb, tb, lb,
    x_sem, leg_sem, f_sem, l_sem, send_sem, recv_sem, own_sem, send2_sem, recv2_sem, own2_sem,
):
    me = lax.axis_index("lat") * NO + lax.axis_index("ord")
    load_x = pltpu.make_async_copy(x_hbm, xs.at[0:LAT], x_sem)
    load_x.start()

    def load_leg(s):
        return pltpu.make_async_copy(leg_hbm.at[s], leg.at[lax.rem(s, 2)], leg_sem.at[lax.rem(s, 2)])

    load_leg(0).start()
    load_leg(1).start()
    greet_signal()
    columns = table_columns(order_ref)
    for s in range(2):
        make_table(s, columns, fb)
    shuffle = shuffle_matrix(False)
    swap = swap_matrix()
    xs[LAT:192] = jnp.zeros((192 - LAT, 16, LON), BF)
    xb[:, :, LON:] = jnp.zeros((PAIRS, 384, LONP - LON), BF)
    load_x.wait()
    fill_grid(xs, xb, swap)
    forward_chunk(0, fb, xb, yb, send, shuffle)
    greet_wait()
    for s in range(2):
        send_slot(s, send, got, send_sem, recv_sem, own_sem)
    for s in range(2, MY):
        make_table(s, columns, fb)
    save_f = pltpu.make_async_copy(fb, f_hbm, f_sem)
    save_f.start()

    def chunk(g, _):
        forward_chunk(g, fb, xb, yb, send, shuffle)
        send_slot(2 * g, send, got, send_sem, recv_sem, own_sem)
        send_slot(2 * g + 1, send, got, send_sem, recv_sem, own_sem)
        return 0

    lax.fori_loop(1, 4, chunk, 0)

    two_part_mixing(mix_ref, mix2)
    split_gain(gain_ref, gp)
    select[...] = lat_select()
    legp[DEG:WIDE, :] = jnp.zeros((WIDE - DEG, WIDE), BF)

    def slot(s, _):
        slot_gain(so_ref[me * MY + s], gp, gs)
        load_leg(s).wait()
        legp[0:DEG, :] = nn(leg[lax.rem(s, 2)], select[...]).astype(BF)

        @pl.when(s + 2 < MY)
        def _():
            load_leg(s + 2).start()

        wait_slot(s, got, recv_sem, own_sem)

        def out(x, v):
            ans[s, x * 16 : x * 16 + 16] = v.reshape(16, 16, 384)

        slot_math(
            lambda x: got[s, x * 16 : x * 16 + 16].reshape(256, 384), legp[...], gs[...], mix2, out
        )
        send_slot(s, ans, ret, send2_sem, recv2_sem, own2_sem)
        return 0

    lax.fori_loop(0, MY, slot, 0)

    shuffle_back = shuffle_matrix(True)

    def save_l(s):
        at = pl.ds(pl.multiple_of(s * 128, 128), 128)
        return pltpu.make_async_copy(
            lb.at[lax.rem(s, 2), 0 : LAT * 16], l_hbm.at[:, at], l_sem.at[lax.rem(s, 2)]
        )

    def back(s, _):
        wait_slot(s, ret, recv2_sem, own2_sem)

        @pl.when(s >= 2)
        def _():
            save_l(s - 2).wait()

        collect(s, ret, bb, tb, lb.at[lax.rem(s, 2)], shuffle_back, swap)
        save_l(s).start()
        return 0

    lax.fori_loop(0, MY, back, 0)
    save_l(MY - 2).wait()
    save_l(MY - 1).wait()
    save_f.wait()
    wait_sent(send, send_sem)
    wait_sent(ans, send2_sem)


def transform(slot_order, degree_gain, mixing, state, legendre):
    vm = pl.BlockSpec(memory_space=pltpu.VMEM)
    hbm = pl.BlockSpec(memory_space=pl.ANY)
    dma = pltpu.SemaphoreType.DMA
    message = pltpu.VMEM((MY, ND, 16, 384), BF)
    return pl.pallas_call(
        transform_kernel,
        out_shape=(
            jax.ShapeDtypeStruct((LAT * 16, 2 * MY * ND), BF),
            jax.ShapeDtypeStruct((2 * MY * ND, LONP), BF),
        ),
        in_specs=[pl.BlockSpec(memory_space=pltpu.SMEM), vm, vm, vm, hbm, hbm],
        out_specs=(hbm, hbm),
        scratch_shapes=[
            pltpu.VMEM((192, 16, LON), BF),
            pltpu.VMEM((PAIRS, 384, LONP), BF),
            pltpu.VMEM((2 * MY * ND, LONP), BF),
            pltpu.VMEM((8, 256, 384), BF),
            message,
            message,
            message,
            message,
            pltpu.VMEM((2, DEG, DEG), BF),
            pltpu.VMEM((WIDE, WIDE), BF),
            pltpu.VMEM((DEG, WIDE), BF),
            pltpu.VMEM((768, WIDE), BF),
            pltpu.VMEM((256, WIDE), F32),
            pltpu.VMEM((512, 512), BF),
            pltpu.VMEM((PAIRS, 128, 384), BF),
            pltpu.VMEM((12, 256, 128), BF),
            pltpu.VMEM((2, 3072, 128), BF),
            dma,
            dma((2,)),
            dma,
            dma((2,)),
            dma,
            dma((MY,)),
            dma((MY,)),
            dma,
            dma((MY,)),
            dma((MY,)),
        ],
        compiler_params=pltpu.CompilerParams(
            collective_id=0, has_side_effects=True, vmem_limit_bytes=VLIM
        ),
        name="transform",
    )(slot_order, slot_order.reshape(ND, MY), degree_gain, mixing, state, legendre)


ROWS = 288


def inverse_kernel(l_ref, f_ref, x_ref, out_ref):
    for n in range(3):
        lanes = slice(n * 512, min(n * 512 + 512, LON))
        back = nn(l_ref[...], f_ref[:, n * 512 : n * 512 + 512])[:, : lanes.stop - lanes.start]
        back = jax.nn.gelu(back, approximate=True)
        out_ref[:, lanes] = (x_ref[:, lanes].astype(F32) + back).astype(BF)


def inverse(l, f, state):
    rows = lambda width: pl.BlockSpec((ROWS, width), lambda i: (i, 0))
    return pl.pallas_call(
        inverse_kernel,
        grid=(LAT * 16 // ROWS,),
        out_shape=jax.ShapeDtypeStruct((LAT * 16, LON), BF),
        in_specs=[rows(2 * MY * ND), pl.BlockSpec(f.shape, lambda i: (0, 0)), rows(LON)],
        out_specs=rows(LON),
        compiler_params=pltpu.CompilerParams(vmem_limit_bytes=VLIM),
        name="inverse",
    )(l, f, state)


def shards(state_field, slot_order, legendre, degree_gain, mixing):
    state = state_field.transpose(1, 0, 2)
    l, f = transform(slot_order, degree_gain, mixing, state, legendre)
    out = inverse(l, f, state.reshape(LAT * 16, LON))
    return out.reshape(LAT, 16, LON).transpose(1, 0, 2)


def solution(mesh):
    placed = (P(("batch", "ord"), "lat", None), P(), P(("lat", "ord"), None, None), P(), P())
    return jax.shard_map(
        shards,
        mesh=mesh,
        in_specs=placed,
        out_specs=P(("batch", "ord"), "lat", None),
        check_vma=False,
    )
```

time: 286 us -> 187 us (0.65)
  Pallas kernels: 258 us -> 185 us
  local copies, waits for them, and re-layouts: 27.6 us -> 1.38 us
    pallas_call x6 -> x2, Pallas kernels: 258 us -> 185 us  [the longest x1 165 us: transform(): pl.pallas_call(transform_kernel, out_shape=(jax.ShapeDtypeStruct((LAT * 1...]
    unnamed x1 -> x0, local copies, waits for them, and re-layouts: 11.9 us -> none
    reshape x3 -> x1, local copies, waits for them, and re-layouts: 10.9 us -> 1.38 us  [transform(): slot_order.reshape(ND, MY)]
where the time goes in v2:
time: 187 us; the launch traced here: 186 us
  Pallas kernels  185 us (99%)
    pallas_call x1, Pallas kernels, transform(): pl.pallas_call(transform_kernel, out_shape=(jax.ShapeDtypeStruct((LAT * 1...  165 us
    pallas_call x1, Pallas kernels, inverse(): pl.pallas_call(inverse_kernel, grid=(LAT * 16 // ROWS,), out_shape=jax.Sh...  19.6 us

profile of v2, /device:TPU:0, one launch (start us, length us, event | category | flops | bytes accessed | tf_op | source)
XLA Modules:
  0.0 186.0 jit_solution(15865266231512113879)
XLA Ops:
  0.0 1.4 reshape.9.order_ref
  1.4 165.1 %transform.1 = (bf16[2880,1024]{1,0:T(8,128)(2,1)}, bf16[1024,1536]{1,0:T(8,128)(2,1)}) custom-call(s32[512]{0:T(512)} %so_ref.1, s32[64,8]{1,0:T(8,128)} %reshape.9.order_ref, f32[720,256]{1,0:T(8,128)} %gain_ref.1, bf16[256,256]{1,0:T(8,128)(2,1)} %mix_ref.1, bf16[180,16,1440]{2,1,0:T(8,128)(2,1)} %bitcast.6, bf16[8,720,720]{2,1,0:T(8,128)(2,1)} %leg_hbm.1), custom_call_target="tpu_custom_call" | custom-call | tf_op jit(solution)/shard_map/transform/pallas_call | solution.py:377
  166.4 19.6 %inverse.1 = bf16[2880,1440]{1,0:T(8,128)(2,1)} custom-call(bf16[2880,1024]{1,0:T(8,128)(2,1)} %get-tuple-element.7.l_ref, bf16[1024,1536]{1,0:T(8,128)(2,1)} %get-tuple-element.8.f_ref, bf16[2880,1440]{1,0:T(8,128)(2,1)} %bitcast.7), custom_call_target="tpu_custom_call" | custom-call | tf_op jit(solution)/shard_map/inverse/pallas_call | solution.py:434

commit v3 on v2

--- a/solution.py
+++ b/solution.py
@@ -168,16 +168,18 @@
     return h * 128 + g * 16 if g < 8 else 256 + h * 64 + (g - 8) * 16
 
 
-def table_columns(order_ref):
-    rep = one_hot(iota((128, ND), 0) // 2 == iota((128, ND), 1))
-    m = order_ref[...]
-    low = nn(rep, (m % 256).astype(F32).astype(BF))
-    high = nn(rep, (m // 256).astype(F32).astype(BF))
-    return low + 256.0 * high
-
-
-def make_table(s, columns, f_ref):
-    m = columns[:, s : s + 1]
+def table_orders(order_ref):
+    d = iota((128, 128), 0) // 2
+    m = jnp.zeros((128, 128), jnp.int32)
+    for i in range(4):
+        m = jnp.where(d // 16 == i, order_ref[i : i + 1, :], m)
+    m = jnp.where(iota((128, 128), 1) // 8 == d % 16, m, 0)
+    return (m % 256).astype(F32).astype(BF), (m // 256).astype(F32).astype(BF)
+
+
+def make_table(s, orders, f_ref):
+    take = one_hot(iota((128, 128), 0) % 8 == s)
+    m = nn(orders[0], take) + 256.0 * nn(orders[1], take)
     r = (iota((128, 1), 0) % 2).astype(F32) * (LON / 4)
     low = m * iota((128, 128), 1).astype(F32) + r
     high = m * (iota((128, 128), 1) * 128).astype(F32)
@@ -189,34 +191,32 @@
         v = c0 * c1[:, t : t + 1] - s0 * s1[:, t : t + 1]
         if t == LONP // 128 - 1:
             v = jnp.where(lane < LON - t * 128, v, 0.0)
-        f_ref[s * 128 : s * 128 + 128, t * 128 : (t + 1) * 128] = v.astype(BF)
-
-
-def fill_grid(xs, xb, swap):
-    def body(g, _):
-        v = nn(swap, xs[pl.ds(g * 16, 16)].reshape(256, LON)).astype(BF)
+        f_ref[pl.ds(pl.multiple_of(s * 128, 128), 128), t * 128 : (t + 1) * 128] = v.astype(BF)
+
+
+def load_grid(g, x_hbm, xs, x_sem):
+    part = pl.ds(g * 16, min(16, LAT - g * 16))
+    return pltpu.make_async_copy(x_hbm.at[part], xs.at[part], x_sem.at[g])
+
+
+def fill_grid(x_hbm, xs, xb, x_sem, swap):
+    for g in range(12):
+        load_grid(g, x_hbm, xs, x_sem).wait()
+        v = nn(swap, xs[g * 16 : g * 16 + 16].reshape(256, LON)).astype(BF)
         for c in range(16):
-            h = c // 8
-            at = jnp.where(g < 8, h * 128 + g * 16, 256 + h * 64 + (g - 8) * 16)
-            xb[c % 8, pl.ds(pl.multiple_of(at, 16), 16), 0:LON] = v[c * 16 : c * 16 + 16]
-        return 0
-
-    lax.fori_loop(0, 12, body, 0)
-
-
-def forward_chunk(g, f_ref, xb, yb, send, shuffle):
-    rows = f_ref[pl.ds(pl.multiple_of(g * 256, 256), 256), :]
-
-    def body(p, _):
+            at = lat_rows(g, c // 8)
+            xb[c % 8, at : at + 16, 0:LON] = v[c * 16 : c * 16 + 16]
+
+
+def forward_slot(s, f_ref, xb, yb, send, shuffle):
+    rows = f_ref[pl.ds(pl.multiple_of(s * 128, 128), 128), :]
+    for p in range(PAIRS):
         y = nt(rows, xb[p]).astype(BF)
-        for q in range(8):
-            yb[q, pl.ds(pl.multiple_of(p * 32, 32), 32), :] = y[q * 32 : q * 32 + 32, :]
-        return 0
-
-    lax.fori_loop(0, PAIRS, body, 0)
-    for q in range(8):
+        for q in range(NX):
+            yb[q, p * 32 : p * 32 + 32, :] = y[q * 32 : q * 32 + 32, :]
+    for q in range(NX):
         v = nn(shuffle, yb[q]).astype(BF)
-        send[2 * g + q // 4, (q % 4) * 16 : (q % 4) * 16 + 16] = v.reshape(16, 16, 384)
+        send[s, q * 16 : q * 16 + 16] = v.reshape(16, 16, 384)
 
 
 def split_gain(gain_ref, gp):
@@ -256,64 +256,73 @@
         for p in range(PAIRS):
             bb[p, x * 32 : x * 32 + 32, :] = v[p * 32 : p * 32 + 32, :]
 
-    def turn(p, _):
+    for p in range(PAIRS):
         t = bb[p].T
         for h in range(2):
             for g in range(12):
                 at = lat_rows(g, h)
-                tb[g, pl.ds(pl.multiple_of(h * 128 + p * 16, 16), 16), :] = t[at : at + 16]
-        return 0
-
-    lax.fori_loop(0, PAIRS, turn, 0)
-
-    def place(g, _):
-        lb[pl.ds(pl.multiple_of(g * 256, 256), 256), :] = nn(swap, tb[g]).astype(BF)
-        return 0
-
-    lax.fori_loop(0, 12, place, 0)
+                tb[g, h * 128 + p * 16 : h * 128 + p * 16 + 16, :] = t[at : at + 16]
+
+    for g in range(12):
+        lb[g * 256 : g * 256 + 256, :] = nn(swap, tb[g]).astype(BF)
+
+
+LAST = MY - 2
+BLOCK = 288
+BLOCKS = LAT * 16 // BLOCK
+
+
+def half_gelu(v):
+    k = math.sqrt(2.0 / math.pi)
+    h = 0.5 * v
+    return h + h * jnp.tanh(v * (k + (k * 0.044715) * (v * v)))
 
 
 def transform_kernel(
     so_ref, order_ref, gain_ref, mix_ref, x_hbm, leg_hbm,
-    l_hbm, f_hbm,
-    xs, xb, fb, yb, send, got, ans, ret, leg, legp, select, gp, gs, mix2, bb, tb, lb,
-    x_sem, leg_sem, f_sem, l_sem, send_sem, recv_sem, own_sem, send2_sem, recv2_sem, own2_sem,
+    part_hbm, l_hbm, f_hbm,
+    fb, send, got, ans, ret, leg, legp, select, gp, gs, mix2, bb, tb, lb,
+    x_sem, leg_sem, out_sem, l_sem, f_sem,
+    send_sem, recv_sem, own_sem, send2_sem, recv2_sem, own2_sem,
 ):
     me = lax.axis_index("lat") * NO + lax.axis_index("ord")
-    load_x = pltpu.make_async_copy(x_hbm, xs.at[0:LAT], x_sem)
-    load_x.start()
+    swap = swap_matrix()
 
     def load_leg(s):
         return pltpu.make_async_copy(leg_hbm.at[s], leg.at[lax.rem(s, 2)], leg_sem.at[lax.rem(s, 2)])
 
-    load_leg(0).start()
-    load_leg(1).start()
-    greet_signal()
-    columns = table_columns(order_ref)
-    for s in range(2):
-        make_table(s, columns, fb)
-    shuffle = shuffle_matrix(False)
-    swap = swap_matrix()
-    xs[LAT:192] = jnp.zeros((192 - LAT, 16, LON), BF)
-    xb[:, :, LON:] = jnp.zeros((PAIRS, 384, LONP - LON), BF)
-    load_x.wait()
-    fill_grid(xs, xb, swap)
-    forward_chunk(0, fb, xb, yb, send, shuffle)
-    greet_wait()
-    for s in range(2):
-        send_slot(s, send, got, send_sem, recv_sem, own_sem)
-    for s in range(2, MY):
-        make_table(s, columns, fb)
-    save_f = pltpu.make_async_copy(fb, f_hbm, f_sem)
-    save_f.start()
-
-    def chunk(g, _):
-        forward_chunk(g, fb, xb, yb, send, shuffle)
-        send_slot(2 * g, send, got, send_sem, recv_sem, own_sem)
-        send_slot(2 * g + 1, send, got, send_sem, recv_sem, own_sem)
-        return 0
-
-    lax.fori_loop(1, 4, chunk, 0)
+    def first(xs, xb, yb):
+        for g in range(12):
+            load_grid(g, x_hbm, xs, x_sem).start()
+        greet_signal()
+        load_leg(0).start()
+        load_leg(1).start()
+        orders = table_orders(order_ref)
+        shuffle = shuffle_matrix(False)
+        xs[LAT:192] = jnp.zeros((192 - LAT, 16, LON), BF)
+        xb[:, :, LON:] = jnp.zeros((PAIRS, 384, LONP - LON), BF)
+        make_table(0, orders, fb)
+        fill_grid(x_hbm, xs, xb, x_sem, swap)
+        greet_wait()
+
+        def slot(s, _):
+            forward_slot(s, fb, xb, yb, send, shuffle)
+            send_slot(s, send, got, send_sem, recv_sem, own_sem)
+
+            @pl.when(s + 1 < MY)
+            def _():
+                make_table(s + 1, orders, fb)
+
+            return 0
+
+        lax.fori_loop(0, MY, slot, 0)
+
+    pl.run_scoped(
+        first,
+        pltpu.VMEM((192, 16, LON), BF),
+        pltpu.VMEM((PAIRS, 384, LONP), BF),
+        pltpu.VMEM((NX, 256, 384), BF),
+    )
 
     two_part_mixing(mix_ref, mix2)
     split_gain(gain_ref, gp)
@@ -342,29 +351,73 @@
 
     lax.fori_loop(0, MY, slot, 0)
 
-    shuffle_back = shuffle_matrix(True)
-
-    def save_l(s):
-        at = pl.ds(pl.multiple_of(s * 128, 128), 128)
-        return pltpu.make_async_copy(
-            lb.at[lax.rem(s, 2), 0 : LAT * 16], l_hbm.at[:, at], l_sem.at[lax.rem(s, 2)]
-        )
-
-    def back(s, _):
-        wait_slot(s, ret, recv2_sem, own2_sem)
-
-        @pl.when(s >= 2)
-        def _():
-            save_l(s - 2).wait()
-
-        collect(s, ret, bb, tb, lb.at[lax.rem(s, 2)], shuffle_back, swap)
-        save_l(s).start()
-        return 0
-
-    lax.fori_loop(0, MY, back, 0)
-    save_l(MY - 2).wait()
-    save_l(MY - 1).wait()
+    save_f = pltpu.make_async_copy(fb.at[LAST * 128 :], f_hbm, f_sem)
+    save_f.start()
+
+    def last(acc, out):
+        shuffle_back = shuffle_matrix(True)
+
+        def block(i):
+            return pl.ds(pl.multiple_of(i * BLOCK, 32), BLOCK)
+
+        def save(i):
+            at = lax.rem(i, 2)
+            return pltpu.make_async_copy(out.at[at], part_hbm.at[block(i)], out_sem.at[at])
+
+        def gather(s, k):
+            wait_slot(s, ret, recv2_sem, own2_sem)
+            collect(s, ret, bb, tb, lb.at[k], shuffle_back, swap)
+
+        def product(t, i, n):
+            v = jnp.concatenate([lb[0, block(i), :], lb[1, block(i), :]], axis=1)
+            rows = pl.ds(pl.multiple_of(t * 256, 256), 256)
+            return nn(v, fb[rows, n * 512 : n * 512 + 512])
+
+        def add(t, start):
+            def body(i, _):
+                for n in range(3):
+                    lanes = slice(n * 512, n * 512 + 512)
+                    v = product(t, i, n)
+                    acc[block(i), lanes] = v if start else acc[block(i), lanes] + v
+                return 0
+
+            lax.fori_loop(0, BLOCKS, body, 0)
+
+        def finish(i, _):
+            @pl.when(i >= 2)
+            def _():
+                save(i - 2).wait()
+
+            for n in range(3):
+                lo, hi = n * 512, min(n * 512 + 512, LON)
+                v = acc[block(i), lo : lo + 512] + product(LAST // 2 - 1, i, n)
+                out[lax.rem(i, 2), :, lo:hi] = v[:, : hi - lo].astype(BF)
+            save(i).start()
+            return 0
+
+        for t in range(LAST // 2):
+            gather(2 * t, 0)
+            gather(2 * t + 1, 1)
+            if t < LAST // 2 - 1:
+                add(t, t == 0)
+        lax.fori_loop(0, BLOCKS, finish, 0)
+        for k in range(2):
+            gather(LAST + k, k)
+            save_l(k).start()
+        save(BLOCKS - 2).wait()
+        save(BLOCKS - 1).wait()
+
+    def save_l(k):
+        return pltpu.make_async_copy(lb.at[k, 0 : LAT * 16], l_hbm.at[k], l_sem.at[k])
+
+    pl.run_scoped(
+        last,
+        pltpu.VMEM((LAT * 16, LONP), F32),
+        pltpu.VMEM((2, BLOCK, LON), BF),
+    )
     save_f.wait()
+    save_l(0).wait()
+    save_l(1).wait()
     wait_sent(send, send_sem)
     wait_sent(ans, send2_sem)
 
@@ -377,16 +430,14 @@
     return pl.pallas_call(
         transform_kernel,
         out_shape=(
-            jax.ShapeDtypeStruct((LAT * 16, 2 * MY * ND), BF),
-            jax.ShapeDtypeStruct((2 * MY * ND, LONP), BF),
+            jax.ShapeDtypeStruct((LAT * 16, LON), BF),
+            jax.ShapeDtypeStruct((2, LAT * 16, 128), BF),
+            jax.ShapeDtypeStruct((256, LONP), BF),
         ),
         in_specs=[pl.BlockSpec(memory_space=pltpu.SMEM), vm, vm, vm, hbm, hbm],
-        out_specs=(hbm, hbm),
+        out_specs=(hbm, hbm, hbm),
         scratch_shapes=[
-            pltpu.VMEM((192, 16, LON), BF),
-            pltpu.VMEM((PAIRS, 384, LONP), BF),
             pltpu.VMEM((2 * MY * ND, LONP), BF),
-            pltpu.VMEM((8, 256, 384), BF),
             message,
             message,
             message,
@@ -400,10 +451,11 @@
             pltpu.VMEM((PAIRS, 128, 384), BF),
             pltpu.VMEM((12, 256, 128), BF),
             pltpu.VMEM((2, 3072, 128), BF),
-            dma,
+            dma((12,)),
+            dma((2,)),
+            dma((2,)),
             dma((2,)),
             dma,
-            dma((2,)),
             dma,
             dma((MY,)),
             dma((MY,)),
@@ -415,37 +467,93 @@
             collective_id=0, has_side_effects=True, vmem_limit_bytes=VLIM
         ),
         name="transform",
-    )(slot_order, slot_order.reshape(ND, MY), degree_gain, mixing, state, legendre)
-
-
-ROWS = 288
-
-
-def inverse_kernel(l_ref, f_ref, x_ref, out_ref):
-    for n in range(3):
-        lanes = slice(n * 512, min(n * 512 + 512, LON))
-        back = nn(l_ref[...], f_ref[:, n * 512 : n * 512 + 512])[:, : lanes.stop - lanes.start]
-        back = jax.nn.gelu(back, approximate=True)
-        out_ref[:, lanes] = (x_ref[:, lanes].astype(F32) + back).astype(BF)
-
-
-def inverse(l, f, state):
-    rows = lambda width: pl.BlockSpec((ROWS, width), lambda i: (i, 0))
+    )(
+        slot_order, slot_order.reshape(4, 128), degree_gain, mixing, state, legendre,
+    )
+
+
+ROWS = 480
+STEPS = LAT * 16 // ROWS
+
+
+def update_kernel(
+    part_hbm, l_hbm, f_hbm, x_hbm, out_hbm,
+    part, l, f, x, out, part_sem, l_sem, f_sem, x_sem, out_sem,
+):
+    def block(i):
+        return pl.ds(pl.multiple_of(i * ROWS, 32), ROWS)
+
+    def loads(i):
+        at = block(i)
+        return (
+            pltpu.make_async_copy(l_hbm.at[:, at], l.at[:, at], l_sem.at[i]),
+            pltpu.make_async_copy(part_hbm.at[at], part.at[at], part_sem.at[i]),
+            pltpu.make_async_copy(x_hbm.at[at], x.at[at], x_sem.at[i]),
+        )
+
+    def save(i):
+        return pltpu.make_async_copy(out.at[block(i)], out_hbm.at[block(i)], out_sem.at[i])
+
+    load_f = pltpu.make_async_copy(f_hbm, f, f_sem)
+    load_f.start()
+    for i in range(2):
+        for copy in loads(i):
+            copy.start()
+    load_f.wait()
+
+    def step(i, _):
+        for copy in loads(i):
+            copy.wait()
+
+        @pl.when(i + 2 < STEPS)
+        def _():
+            for copy in loads(i + 2):
+                copy.start()
+
+        at = block(i)
+        rows = jnp.concatenate([l[0, at, :], l[1, at, :]], axis=1)
+        for n in range(3):
+            lo, hi = n * 512, min(n * 512 + 512, LON)
+            v = nn(rows, f[:, lo : lo + 512])[:, : hi - lo] + part[at, lo:hi].astype(F32)
+            out[at, lo:hi] = (x[at, lo:hi].astype(F32) + half_gelu(v)).astype(BF)
+        save(i).start()
+        return 0
+
+    lax.fori_loop(0, STEPS, step, 0)
+    for i in range(STEPS):
+        save(i).wait()
+
+
+def update(part, l, f, state):
+    hbm = pl.BlockSpec(memory_space=pl.ANY)
+    dma = pltpu.SemaphoreType.DMA
+    whole = pltpu.VMEM((LAT * 16, LON), BF)
     return pl.pallas_call(
-        inverse_kernel,
-        grid=(LAT * 16 // ROWS,),
+        update_kernel,
         out_shape=jax.ShapeDtypeStruct((LAT * 16, LON), BF),
-        in_specs=[rows(2 * MY * ND), pl.BlockSpec(f.shape, lambda i: (0, 0)), rows(LON)],
-        out_specs=rows(LON),
+        in_specs=[hbm] * 4,
+        out_specs=hbm,
+        scratch_shapes=[
+            whole,
+            pltpu.VMEM(l.shape, BF),
+            pltpu.VMEM(f.shape, BF),
+            whole,
+            whole,
+            dma((STEPS,)),
+            dma((STEPS,)),
+            dma,
+            dma((STEPS,)),
+            dma((STEPS,)),
+        ],
         compiler_params=pltpu.CompilerParams(vmem_limit_bytes=VLIM),
-        name="inverse",
-    )(l, f, state)
+        name="update",
+    )(part, l, f, state)
 
 
 def shards(state_field, slot_order, legendre, degree_gain, mixing):
     state = state_field.transpose(1, 0, 2)
-    l, f = transform(slot_order, degree_gain, mixing, state, legendre)
-    out = inverse(l, f, state.reshape(LAT * 16, LON))
+    part, l, f = transform(slot_order, degree_gain, mixing, state, legendre)
+    out = update(part, l, f, state.reshape(LAT * 16, LON))
     return out.reshape(LAT, 16, LON).transpose(1, 0, 2)
 
 

time: 187 us -> 172 us (0.920)
  Pallas kernels: 185 us -> 171 us
    pallas_call x1, Pallas kernels: 19.6 us -> 12.3 us  [update(): pl.pallas_call(update_kernel, out_shape=jax.ShapeDtypeStruct((LAT * 16, L...]
    pallas_call x1, Pallas kernels: 165 us -> 159 us  [transform(): pl.pallas_call(transform_kernel, out_shape=(jax.ShapeDtypeStruct((LAT * 1...]
where the time goes in v3:
time: 172 us
  Pallas kernels  171 us (99%)
    pallas_call x1, Pallas kernels, transform(): pl.pallas_call(transform_kernel, out_shape=(jax.ShapeDtypeStruct((LAT * 1...  159 us
    pallas_call x1, Pallas kernels, update(): pl.pallas_call(update_kernel, out_shape=jax.ShapeDtypeStruct((LAT * 16, L...  12.3 us

profile of v3, /device:TPU:0, one launch (start us, length us, event | category | flops | bytes accessed | tf_op | source)
XLA Modules:
  0.0 171.6 jit_solution(12234480109853735240)
XLA Ops:
  0.0 159.2 %transform.1 = (bf16[2880,1440]{1,0:T(8,128)(2,1)}, bf16[2,2880,128]{2,1,0:T(8,128)(2,1)}, bf16[256,1536]{1,0:T(8,128)(2,1)}) custom-call(s32[512]{0:T(512)} %so_ref.1, s32[4,128]{1,0:T(4,128)} %bitcast.9, f32[720,256]{1,0:T(8,128)} %gain_ref.1, bf16[256,256]{1,0:T(8,128)(2,1)} %mix_ref.1, bf16[180,16,1440]{2,1,0:T(8,128)(2,1)} %bitcast.7, ...), custom_call_target="tpu_custom_call" | custom-call | tf_op jit(solution)/shard_map/transform/pallas_call | solution.py:430
  159.2 12.3 %update.1 = bf16[2880,1440]{1,0:T(8,128)(2,1)} custom-call(bf16[2880,1440]{1,0:T(8,128)(2,1)} %get-tuple-element.8.part_hbm, bf16[2,2880,128]{2,1,0:T(8,128)(2,1)} %get-tuple-element.9.l_hbm, bf16[256,1536]{1,0:T(8,128)(2,1)} %get-tuple-element.10.f_hbm, bf16[2880,1440]{1,0:T(8,128)(2,1)} %bitcast.8), custom_call_target="tpu_custom_call" | custom-call | tf_op jit(solution)/shard_map/update/pallas_call | solution.py:531

commit v4 on v3

--- a/solution.py
+++ b/solution.py
@@ -194,6 +194,9 @@
         f_ref[pl.ds(pl.multiple_of(s * 128, 128), 128), t * 128 : (t + 1) * 128] = v.astype(BF)
 
 
+DEEP = 4
+
+
 def load_grid(g, x_hbm, xs, x_sem):
     part = pl.ds(g * 16, min(16, LAT - g * 16))
     return pltpu.make_async_copy(x_hbm.at[part], xs.at[part], x_sem.at[g])
@@ -202,6 +205,8 @@
 def fill_grid(x_hbm, xs, xb, x_sem, swap):
     for g in range(12):
         load_grid(g, x_hbm, xs, x_sem).wait()
+        if g + DEEP < 12:
+            load_grid(g + DEEP, x_hbm, xs, x_sem).start()
         v = nn(swap, xs[g * 16 : g * 16 + 16].reshape(256, LON)).astype(BF)
         for c in range(16):
             at = lat_rows(g, c // 8)
@@ -234,7 +239,7 @@
 def slot_gain(m, gp, gs):
     pick = one_hot(iota((WIDE, WIDE), 0) == iota((WIDE, WIDE), 1) + m)
     v = nn(gp[...], pick)
-    weight = jnp.where(jnp.full((1, WIDE), m, jnp.int32) == 0, 1.0, 2.0)
+    weight = jnp.where(jnp.full((1, WIDE), m, jnp.int32) == 0, 0.5, 1.0)
     gs[...] = (v[0:256] + v[256:512] + v[512:768]) * weight
 
 
@@ -272,29 +277,32 @@
 BLOCKS = LAT * 16 // BLOCK
 
 
-def half_gelu(v):
-    k = math.sqrt(2.0 / math.pi)
-    h = 0.5 * v
-    return h + h * jnp.tanh(v * (k + (k * 0.044715) * (v * v)))
+def gelu_of_half(h):
+    k = 2.0 * math.sqrt(2.0 / math.pi)
+    return h + h * jnp.tanh(h * (k + (k * 4.0 * 0.044715) * (h * h)))
 
 
 def transform_kernel(
-    so_ref, order_ref, gain_ref, mix_ref, x_hbm, leg_hbm,
+    so_ref, order_ref, gain_hbm, mix_hbm, x_hbm, leg_hbm,
     part_hbm, l_hbm, f_hbm,
-    fb, send, got, ans, ret, leg, legp, select, gp, gs, mix2, bb, tb, lb,
-    x_sem, leg_sem, out_sem, l_sem, f_sem,
+    gain, mix, fb, send, got, ans, ret, leg, legp, select, gp, gs, mix2, bb, tb, lb,
+    gain_sem, mix_sem, x_sem, leg_sem, out_sem, l_sem, f_sem,
     send_sem, recv_sem, own_sem, send2_sem, recv2_sem, own2_sem,
 ):
     me = lax.axis_index("lat") * NO + lax.axis_index("ord")
     swap = swap_matrix()
+    load_gain = pltpu.make_async_copy(gain_hbm, gain, gain_sem)
+    load_mix = pltpu.make_async_copy(mix_hbm, mix, mix_sem)
 
     def load_leg(s):
         return pltpu.make_async_copy(leg_hbm.at[s], leg.at[lax.rem(s, 2)], leg_sem.at[lax.rem(s, 2)])
 
     def first(xs, xb, yb):
-        for g in range(12):
+        for g in range(DEEP):
             load_grid(g, x_hbm, xs, x_sem).start()
         greet_signal()
+        load_gain.start()
+        load_mix.start()
         load_leg(0).start()
         load_leg(1).start()
         orders = table_orders(order_ref)
@@ -324,8 +332,10 @@
         pltpu.VMEM((NX, 256, 384), BF),
     )
 
-    two_part_mixing(mix_ref, mix2)
-    split_gain(gain_ref, gp)
+    load_mix.wait()
+    two_part_mixing(mix, mix2)
+    load_gain.wait()
+    split_gain(gain, gp)
     select[...] = lat_select()
     legp[DEG:WIDE, :] = jnp.zeros((WIDE - DEG, WIDE), BF)
 
@@ -434,9 +444,11 @@
             jax.ShapeDtypeStruct((2, LAT * 16, 128), BF),
             jax.ShapeDtypeStruct((256, LONP), BF),
         ),
-        in_specs=[pl.BlockSpec(memory_space=pltpu.SMEM), vm, vm, vm, hbm, hbm],
+        in_specs=[pl.BlockSpec(memory_space=pltpu.SMEM), vm, hbm, hbm, hbm, hbm],
         out_specs=(hbm, hbm, hbm),
         scratch_shapes=[
+            pltpu.VMEM((DEG, 256), F32),
+            pltpu.VMEM((256, 256), BF),
             pltpu.VMEM((2 * MY * ND, LONP), BF),
             message,
             message,
@@ -451,6 +463,8 @@
             pltpu.VMEM((PAIRS, 128, 384), BF),
             pltpu.VMEM((12, 256, 128), BF),
             pltpu.VMEM((2, 3072, 128), BF),
+            dma,
+            dma,
             dma((12,)),
             dma((2,)),
             dma((2,)),
@@ -515,7 +529,7 @@
         for n in range(3):
             lo, hi = n * 512, min(n * 512 + 512, LON)
             v = nn(rows, f[:, lo : lo + 512])[:, : hi - lo] + part[at, lo:hi].astype(F32)
-            out[at, lo:hi] = (x[at, lo:hi].astype(F32) + half_gelu(v)).astype(BF)
+            out[at, lo:hi] = (x[at, lo:hi].astype(F32) + gelu_of_half(v)).astype(BF)
         save(i).start()
         return 0
 

time: 172 us -> 171 us (level)
  no operation moved by 1% of the time
where the time goes in v4:
time: 171 us
  Pallas kernels  171 us (100%)
    pallas_call x1, Pallas kernels, transform(): pl.pallas_call(transform_kernel, out_shape=(jax.ShapeDtypeStruct((LAT * 1...  159 us
    pallas_call x1, Pallas kernels, update(): pl.pallas_call(update_kernel, out_shape=jax.ShapeDtypeStruct((LAT * 16, L...  11.9 us

profile of v4, /device:TPU:0, one launch (start us, length us, event | category | flops | bytes accessed | tf_op | source)
XLA Modules:
  0.0 170.8 jit_solution(4594935407288642041)
XLA Ops:
  0.0 158.7 %transform.1 = (bf16[2880,1440]{1,0:T(8,128)(2,1)}, bf16[2,2880,128]{2,1,0:T(8,128)(2,1)}, bf16[256,1536]{1,0:T(8,128)(2,1)}) custom-call(s32[512]{0:T(512)} %so_ref.1, s32[4,128]{1,0:T(4,128)} %bitcast.9, f32[720,256]{1,0:T(8,128)} %gain_hbm.1, bf16[256,256]{1,0:T(8,128)(2,1)} %mix_hbm.1, bf16[180,16,1440]{2,1,0:T(8,128)(2,1)} %bitcast.7, ...), custom_call_target="tpu_custom_call" | custom-call | tf_op jit(solution)/shard_map/transform/pallas_call | solution.py:440
  158.7 11.9 %update.1 = bf16[2880,1440]{1,0:T(8,128)(2,1)} custom-call(bf16[2880,1440]{1,0:T(8,128)(2,1)} %get-tuple-element.8.part_hbm, bf16[2,2880,128]{2,1,0:T(8,128)(2,1)} %get-tuple-element.9.l_hbm, bf16[256,1536]{1,0:T(8,128)(2,1)} %get-tuple-element.10.f_hbm, bf16[2880,1440]{1,0:T(8,128)(2,1)} %bitcast.8), custom_call_target="tpu_custom_call" | custom-call | tf_op jit(solution)/shard_map/update/pallas_call | solution.py:545
